TPU v7x, 32 devices: a whole 2x2x4 slice. The times are simulated.
32 devices in a mesh: ep: 16 (over z, x, core), dp: 2 (over y).
Axes of the slice: x: 2, y: 2, z: 4, core: 2. Of those that a mesh axis runs over, the one named last changes fastest.
Arguments:
- tokens: bfloat16 [2048, 1024], P(('dp', 'ep')), parts along dimension 0, may hold values from -6 to 6
- norm_gain: float32 [1024], replicated, may hold values from 0.1 to 1.9
- router_weight: bfloat16 [1024, 16], replicated, may hold values from -0.1875 to 0.1875
- expert_ids: int32 [2048, 2], P(('dp', 'ep')), parts along dimension 0, may hold values from 0 to 15, all different within a row; in each aligned block of 64 rows (0 to 63, 64 to 127, ...) at most 32 rows name the same one
- w_gate: bfloat16 [16, 1024, 512], P('ep'), may hold values from -0.1875 to 0.1875
- w_up: bfloat16 [16, 1024, 512], P('ep'), may hold values from -0.1875 to 0.1875
- w_down: bfloat16 [16, 512, 1024], P('ep'), may hold values from -0.25 to 0.25
Outputs:
- moe_out: bfloat16 [2048, 1024], P(('dp', 'ep')), parts along dimension 0
There are 2 independent parts, one for each index of `dp`. A program takes and returns all parts, laid end to end along the dimension named above; an argument that names none is the same for every part. Nothing has to cross between parts.
Inputs may be any that keep to these rules, and one draw needn't show every extreme that they name: Each row of expert_ids names 2 different experts of 0 to 15; within the rows of one device (aligned blocks of 64 rows) no expert is named more than 32 times, and in some block one expert is named exactly 32 times.
All inputs are finite; a program needn't handle non-finite values.
Results may differ from a plain program's by a relative error of at most 0.0015.
Values may be sent and summed in bfloat16 or wider, within the bound.
A program may use at most 64 MiB of HBM per device.

v0:
```python
import jax
import jax.numpy as jnp
from jax import lax
from jax.sharding import PartitionSpec as P

epsilon = 1e-05


def normalize(tokens, norm_gain):
    values = tokens.astype(jnp.float32)
    inverse = lax.rsqrt(jnp.mean(values * values, axis=1, keepdims=True) + epsilon)
    return (values * inverse * norm_gain).astype(jnp.bfloat16)


def gate_values(normed, router_weight, expert_ids):
    logits = jnp.dot(normed, router_weight, preferred_element_type=jnp.float32)
    chosen = jnp.take_along_axis(logits, expert_ids, axis=1)
    return jax.nn.softmax(chosen, axis=1)


def expert_output(block_rows, gate_matrix, up_matrix, down_matrix):
    gate_part = jnp.dot(block_rows, gate_matrix, preferred_element_type=jnp.float32)
    up_part = jnp.dot(block_rows, up_matrix, preferred_element_type=jnp.float32)
    hidden = (jax.nn.silu(gate_part) * up_part).astype(jnp.bfloat16)
    return jnp.dot(hidden, down_matrix, preferred_element_type=jnp.float32)


def shards(tokens, norm_gain, router_weight, expert_ids, w_gate, w_up, w_down):
    normed = normalize(tokens, norm_gain)
    token_gates = gate_values(normed, router_weight, expert_ids)
    cycle_size = lax.axis_size("ep")
    tok_rows = normed.shape[0]
    width = normed.shape[1]
    top_count = expert_ids.shape[1]
    expert_total = router_weight.shape[1]
    local_count = w_gate.shape[0]
    capacity = max(1, min(tok_rows, 4 * tok_rows * top_count // expert_total))
    choice_rows = tok_rows * top_count
    flat_ids = expert_ids.reshape(choice_rows).astype(jnp.int32)
    numbers = jnp.arange(expert_total, dtype=jnp.int32)
    onehot = (flat_ids[:, None] == numbers[None, :]).astype(jnp.int32)
    earlier = jnp.cumsum(onehot, axis=0) - onehot
    slot = jnp.sum(earlier * onehot, axis=1)
    target = (flat_ids * capacity + slot).astype(jnp.int32)
    source_row = jnp.zeros((expert_total * capacity,), jnp.int32)
    source_row = source_row.at[target].set(jnp.arange(choice_rows, dtype=jnp.int32) + 1)
    repeated = jnp.repeat(normed, top_count, axis=0)
    padded = jnp.concatenate([jnp.zeros((1, width), jnp.bfloat16), repeated], axis=0)
    outgoing = padded[source_row].reshape(cycle_size, local_count, capacity, width)
    arrived = lax.all_to_all(outgoing, "ep", split_axis=0, concat_axis=0, tiled=True)
    produced_list = []
    for within in range(local_count):
        rows_in = arrived[:, within].reshape(cycle_size * capacity, width)
        produced = expert_output(rows_in, w_gate[within], w_up[within], w_down[within])
        produced_list.append(produced.reshape(cycle_size, capacity, width))
    produced_all = jnp.stack(produced_list, axis=1)
    back = lax.all_to_all(produced_all, "ep", split_axis=0, concat_axis=0, tiled=True)
    back = back.reshape(expert_total * capacity, width)
    picked = back[target].reshape(tok_rows, top_count, width)
    finished = jnp.sum(token_gates[:, :, None] * picked, axis=1)
    return finished.astype(jnp.bfloat16)


def solution(mesh):
    return jax.shard_map(
        shards,
        mesh=mesh,
        in_specs=(
            P(("dp", "ep"), None),
            P(),
            P(),
            P(("dp", "ep"), None),
            P("ep", None, None),
            P("ep", None, None),
            P("ep", None, None),
        ),
        out_specs=P(("dp", "ep"), None),
        check_vma=False,
    )
```

profile of v0, /device:TPU:11, one launch (start us, length us, event | category | flops | bytes accessed | tf_op | source)
XLA Modules:
  0.0 100.3 jit_solution(17863457023799391209)
XLA Ops:
  0.0 0.0 copy-start
  0.0 0.8 broadcast_multiply_fusion
  0.8 0.8 copy.41
  1.5 1.0 %fusion.5 = f32[64]{0:T(128)S(1)} fusion(bf16[64,1024]{1,0:T(8,128)(2,1)} %param.7), kind=kLoop, calls=%fused_computation.14 | loop fusion | flops 196544 | bytes 131328 | tf_op jit(solution)/shard_map/reduce_sum | solution.py:11
  2.6 0.1 copy.40
  2.7 0.1 mul.61
  2.8 0.1 eq.15
  3.0 0.1 fusion.8
  3.1 0.2 reduce_window_sum.11
  3.2 0.2 select_reduce_fusion
  3.4 1.0 scatter_custom_fusion
  4.4 1.0 %fusion.7 = bf16[64,1024]{1,0:T(8,128)(2,1)S(1)} fusion(bf16[64,1024]{1,0:T(8,128)(2,1)} %param.7, f32[1024]{0:T(1024)} %param.8, f32[64]{0:T(128)S(1)} %add_rsqrt_fusion), kind=kLoop, calls=%fused_computation.16 | loop fusion | flops 262144 | bytes 266496 | tf_op jit(solution)/shard_map/convert_element_type | solution.py:12
  5.5 0.1 broadcast_in_dim.9
  5.6 0.1 reshape.87
  5.7 0.1 concatenate.3
  5.8 2.1 %gather_fusion = bf16[512,1024]{1,0:T(8,128)(2,1)S(1)} fusion(bf16[129,1024]{1,0:T(8,128)(2,1)S(1)} %concatenate.3, s32[1024]{0:T(1024)S(1)} %pad_clamp_fusion.1), kind=kCustom, calls=%fused_computation | custom fusion | bytes 2099200 | tf_op jit(solution)/shard_map/gather | solution.py:49
  7.9 0.0 copy-start.3
  7.9 31.6 %all_to_all.10 = bf16[16,1,32,1024]{3,2,1,0:T(8,128)(2,1)S(1)} all-to-all(bf16[16,1,32,1024]{3,2,1,0:T(8,128)(2,1)S(1)} %bitcast.37), channel_id=1, replica_groups=mesh['ep'=16,'dp'=2] {'ep'}, dimensions={0} | all-to-all | bytes 2097152 | tf_op jit(solution)/shard_map/all_to_all | solution.py:50
  39.5 0.0 copy-start.4
  39.5 0.0 copy-done.3
  39.5 0.7 fusion.3
  40.2 0.5 copy-done.4
  40.7 0.8 fusion
  41.5 0.0 copy-done
  41.5 2.1 %convolution_bitcast_fusion = f32[16,1,32,1024]{3,2,1,0:T(8,128)} fusion(bf16[16,32,512]{2,1,0:T(8,128)(2,1)S(1)} %bitcast.40, bf16[1,512,1024]{2,1,0:T(8,128)(2,1)S(1)} %copy-done), kind=kOutput, calls=%fused_computation.4 | convolution fusion | flops 536870912 | bytes 3670016 | tf_op jit(solution)/shard_map/dot_general | solution.py:25
  43.6 0.0 copy-start.2
  43.6 0.0 copy-start.1
  43.6 4.5 %all-to-all-start.1 = ((f32[16,1,32,1024]{3,2,1,0:T(8,128)}), f32[16,1,32,1024]{3,2,1,0:T(8,128)S(1)}, u32[]{:S(2)}, u32[]{:S(2)}) async-start(f32[16,1,32,1024]{3,2,1,0:T(8,128)} %convolution_bitcast_fusion), calls=%async_computation.1 | async-start | bytes 4194304 | tf_op jit(solution)/shard_map/all_to_all | solution.py:57
  48.1 0.0 copy-done.2
  48.1 0.1 copy.37
  48.2 0.1 reshape.108
  48.3 0.0 copy-done.1
  48.4 0.1 fusion.15
  48.5 1.3 %gather_fusion.2 = f32[128]{0:T(128)S(1)} fusion(f32[64,16]{0,1:T(8,128)S(1)} %fusion.15, s32[128]{0:T(128)S(1)} %reshape.108), kind=kCustom, calls=%fused_computation.2 | custom fusion | bytes 2048 | tf_op jit(solution)/shard_map/jit(take_along_axis)/gather | solution.py:17
  49.8 0.1 reshape.111
  50.0 0.1 copy.38
  50.1 0.1 copy.39
  50.2 45.8 %all-to-all-done.1 = f32[16,1,32,1024]{3,2,1,0:T(8,128)S(1)} async-done(((f32[16,1,32,1024]{3,2,1,0:T(8,128)}), f32[16,1,32,1024]{3,2,1,0:T(8,128)S(1)}, u32[]{:S(2)}, u32[]{:S(2)}) %all-to-all-start.1) | async-done | bytes 2097184 | tf_op jit(solution)/shard_map/all_to_all | solution.py:57
  96.0 1.6 %gather_fusion.1 = f32[128,1024]{1,0:T(8,128)} fusion(f32[512,1024]{1,0:T(8,128)S(1)} %bitcast.36, s32[1024]{0:T(1024)S(1)} %pad_clamp_fusion), kind=kCustom, calls=%fused_computation.1 | custom fusion | bytes 1049088 | tf_op jit(solution)/shard_map/gather | solution.py:59
  97.6 1.3 %reshape.91 = f32[64,2,1024]{2,1,0:T(2,128)S(1)} reshape(f32[128,1024]{1,0:T(8,128)} %gather_fusion.1) | data formatting | bytes 1048576 | tf_op jit(solution)/shard_map/reshape | solution.py:59
  99.0 1.4 %multiply_reduce_fusion = bf16[64,1024]{1,0:T(8,128)(2,1)} fusion(f32[64,2,1024]{2,1,0:T(2,128)S(1)} %reshape.91, f32[64,2]{1,0:T(8,128)S(1)} %copy.39), kind=kLoop, calls=%fused_computation.11 | loop fusion | flops 196608 | bytes 655872 | tf_op jit(solution)/shard_map/reduce_sum | solution.py:60
  (10 shorter events, 0.1 us)
Async XLA Ops:
  0.0 41.5 %copy-start = (bf16[1,512,1024]{2,1,0:T(8,128)(2,1)S(1)}, bf16[1,512,1024]{2,1,0:T(8,128)(2,1)}, u32[]{:S(2)}) copy-start(bf16[1,512,1024]{2,1,0:T(8,128)(2,1)} %param.13) | copy-start | bytes 3145732
  7.9 31.7 %copy-start.3 = (bf16[1,1024,512]{2,1,0:T(8,128)(2,1)S(1)}, bf16[1,1024,512]{2,1,0:T(8,128)(2,1)}, u32[]{:S(2)}) copy-start(bf16[1,1024,512]{2,1,0:T(8,128)(2,1)} %param.11) | copy-start | bytes 3145732
  39.5 1.2 %copy-start.4 = (bf16[1,1024,512]{2,1,0:T(8,128)(2,1)S(1)}, bf16[1,1024,512]{2,1,0:T(8,128)(2,1)}, u32[]{:S(2)}) copy-start(bf16[1,1024,512]{2,1,0:T(8,128)(2,1)} %param.12) | copy-start | bytes 3145732
  43.6 4.5 %copy-start.2 = (s32[64,2]{0,1:T(2,128)S(1)}, s32[64,2]{0,1:T(2,128)}, u32[]{:S(2)}) copy-start(s32[64,2]{0,1:T(2,128)} %param.10) | copy-start | bytes 1540
  43.6 4.7 %copy-start.1 = (bf16[1024,16]{0,1:T(8,128)(2,1)S(1)}, bf16[1024,16]{0,1:T(8,128)(2,1)}, u32[]{:S(2)}) copy-start(bf16[1024,16]{0,1:T(8,128)(2,1)} %param.9) | copy-start | bytes 98308
  43.6 52.4 %all-to-all-start.1 = ((f32[16,1,32,1024]{3,2,1,0:T(8,128)}), f32[16,1,32,1024]{3,2,1,0:T(8,128)S(1)}, u32[]{:S(2)}, u32[]{:S(2)}) async-start(f32[16,1,32,1024]{3,2,1,0:T(8,128)} %convolution_bitcast_fusion), calls=%async_computation.1 | async-start | bytes 4194304 | tf_op jit(solution)/shard_map/all_to_all | solution.py:57
where the time goes:
time: 101 us; the launch traced here: 100 us
  waiting for transfers between devices  45.8 us (45%)
  blocking collectives  31.6 us (31%)
  local copies, waits for them, and re-layouts  9.79 us (10%)
  other arithmetic  4.72 us (5%)
  starting transfers between devices  4.49 us (4%)
  matrix products  3.7 us (4%)
    all_to_all x1, waiting for transfers between devices, shards(): lax.all_to_all(produced_all, 'ep', split_axis=0, concat_axis=0, tiled=True)  45.8 us
    all_to_all x1, blocking collectives, shards(): lax.all_to_all(outgoing, 'ep', split_axis=0, concat_axis=0, tiled=True)  31.6 us
    all_to_all x1, starting transfers between devices, shards(): lax.all_to_all(produced_all, 'ep', split_axis=0, concat_axis=0, tiled=True)  4.49 us
    dot_general x1, matrix products, expert_output(): return jnp.dot(hidden, down_matrix, preferred_element_type=jnp.float32)  2.07 us
    gather x1, local copies, waits for them, and re-layouts, shards(): padded[source_row].reshape(cycle_size, local_count, capacity, width)  2.06 us
  transfers between devices with their start and end apart: 1, of which 1 were waited for; matrix products, arithmetic and copies ran while one was open for 2% of the time, Pallas kernels for 0%

commit v1 on v0

v1 whole, which is shorter than its diff:
```python
import jax
import jax.numpy as jnp
from jax import lax
from jax.sharding import PartitionSpec as P

epsilon = 1e-05


def normalize(tokens, norm_gain):
    values = tokens.astype(jnp.float32)
    inverse = lax.rsqrt(jnp.mean(values * values, axis=1, keepdims=True) + epsilon)
    return (values * inverse * norm_gain).astype(jnp.bfloat16)


def combine_of(normed, router_weight, expert_ids, expert):
    logits = jnp.dot(normed, router_weight, preferred_element_type=jnp.float32)
    numbers = lax.broadcasted_iota(jnp.int32, logits.shape, 1)
    hits = [numbers == expert_ids[:, k:k + 1] for k in range(expert_ids.shape[1])]
    chosen = jnp.stack([jnp.sum(jnp.where(h, logits, 0.0), axis=1) for h in hits], axis=1)
    gates = jax.nn.softmax(chosen, axis=1)
    return jnp.sum(jnp.where(expert_ids == expert, gates, 0.0), axis=1, keepdims=True)


def expert_output(block_rows, gate_matrix, up_matrix, down_matrix):
    gate_part = jnp.dot(block_rows, gate_matrix, preferred_element_type=jnp.float32)
    up_part = jnp.dot(block_rows, up_matrix, preferred_element_type=jnp.float32)
    hidden = (jax.nn.silu(gate_part) * up_part).astype(jnp.bfloat16)
    return jnp.dot(hidden, down_matrix, preferred_element_type=jnp.float32)


def shards(tokens, norm_gain, router_weight, expert_ids, w_gate, w_up, w_down):
    local_count = w_gate.shape[0]
    me = lax.axis_index("ep")
    normed = normalize(tokens, norm_gain)
    all_rows = lax.all_gather(normed, "ep", axis=0, tiled=True)
    all_ids = lax.all_gather(expert_ids, "ep", axis=0, tiled=True)
    total = None
    for within in range(local_count):
        weight = combine_of(all_rows, router_weight, all_ids, me * local_count + within)
        produced = expert_output(all_rows, w_gate[within], w_up[within], w_down[within])
        term = jnp.where(weight > 0, weight * produced, 0.0)
        total = term if total is None else total + term
    finished = lax.psum_scatter(total, "ep", scatter_dimension=0, tiled=True)
    return finished.astype(jnp.bfloat16)


def solution(mesh):
    return jax.shard_map(
        shards,
        mesh=mesh,
        in_specs=(
            P(("dp", "ep"), None),
            P(),
            P(),
            P(("dp", "ep"), None),
            P("ep", None, None),
            P("ep", None, None),
            P("ep", None, None),
        ),
        out_specs=P(("dp", "ep"), None),
        check_vma=False,
    )
```

time: 101 us -> 147 us (1.46)
  the two profiles are of different devices: /device:TPU:11 before, /device:TPU:0 now
where the time goes in v1:
time: 147 us
  waiting for transfers between devices  92.7 us (63%)
  blocking collectives  23.4 us (16%)
  between operations  13.5 us (9%)
  matrix products  12.5 us (9%)
  other arithmetic  4.49 us (3%)
    reduce_scatter x1, waiting for transfers between devices, shards(): finished = lax.psum_scatter(total, 'ep', scatter_dimension=0, tiled=True)  71.6 us
    all_gather x1, blocking collectives, shards(): all_ids = lax.all_gather(expert_ids, 'ep', axis=0, tiled=True)  23.4 us
    all_gather x1, waiting for transfers between devices, shards(): all_rows = lax.all_gather(normed, 'ep', axis=0, tiled=True)  21 us
    dot_general x1, matrix products, expert_output(): return jnp.dot(hidden, down_matrix, preferred_element_type=jnp.float32)  6.28 us
    dot_general x1, matrix products, expert_output(): jnp.dot(block_rows, gate_matrix, preferred_element_type=jnp.float32)  3.81 us
  transfers between devices with their start and end apart: 2, of which 2 were waited for; matrix products, arithmetic and copies ran while one was open for 0% of the time, Pallas kernels for 0%

profile of v1, /device:TPU:0, one launch (start us, length us, event | category | flops | bytes accessed | tf_op | source)
XLA Modules:
  0.0 146.7 jit_solution(1392610962845810464)
XLA Ops:
  6.5 0.0 copy-start
  6.5 0.0 all-gather.3.cloned.1.call-start
  6.5 1.1 fusion.6
  7.7 1.7 %fusion.8 = bf16[64,1024]{1,0:T(8,128)(2,1)} fusion(bf16[64,1024]{1,0:T(8,128)(2,1)} %param.7, f32[1024]{0:T(1024)} %param.8, f32[64]{0:T(128)S(1)} %add_rsqrt_fusion), kind=kLoop, calls=%fused_computation.10 | loop fusion | flops 262144 | bytes 266496 | tf_op jit(solution)/shard_map/convert_element_type | solution.py:12
  9.3 0.0 all-gather.3.cloned.1.call-update
  9.4 0.0 reduce-scatter.2.cloned.1.call-start
  9.4 23.4 %all-gather = s32[16,64,2]{1,2,0:T(2,128)S(1)} all-gather(s32[1,64,2]{1,2,0:T(2,128)} %bitcast.28), channel_id=1, replica_groups=mesh['ep'=16,'dp'=2] {'ep'}, dimensions={0}, use_global_device_ids=true | all-gather | bytes 8704 | tf_op jit(solution)/shard_map/all_gather | solution.py:36
  32.8 0.1 reshape.25
  32.9 21.0 %all-gather.3.cloned.1.call-done = bf16[1024,1024]{1,0:T(8,128)(2,1)} async-done(((bf16[64,1024]{1,0:T(8,128)(2,1)}), bf16[1024,1024]{1,0:T(8,128)(2,1)}) %all-gather.3.cloned.1.call-update) | async-done | bytes 2097168 | tf_op jit(solution)/shard_map/all_gather | solution.py:35
  54.0 0.0 copy-start.1
  54.0 2.4 %select_reduce_fusion = (f32[1024]{0:T(1024)S(1)}, f32[1024]{0:T(1024)S(1)}) fusion(s32[1024]{0:T(1024)S(1)} %bitcast.27, s32[1024]{0:T(1024)S(1)} %bitcast.26, bf16[1024,1024]{1,0:T(8,128)(2,1)} %all-gather.3.cloned.1.call-done, bf16[1024,16]{0,1:T(8,128)(2,1)} %param.9), kind=kOutput, calls=%fused_computation.11 | convolution fusion | flops 33650688 | bytes 2146304 | tf_op jit(solution)/shard_map/dot_general | solution.py:16
  56.5 0.0 copy-done.1
  56.5 3.8 %fusion.2 = f32[1024,512]{1,0:T(8,128)} fusion(bf16[1024,1024]{1,0:T(8,128)(2,1)S(1)} %copy-done.1, bf16[1,1024,512]{2,1,0:T(8,128)(2,1)} %param.11), kind=kOutput, calls=%fused_computation.4 | convolution fusion | flops 1073741824 | bytes 5242880 | tf_op jit(solution)/shard_map/dot_general | solution.py:25
  60.3 0.0 copy-done
  60.3 6.3 %multiply_select_fusion = f32[1024,1024]{1,0:T(8,128)} fusion(f32[1024]{0:T(1024)S(1)} %fusion.10, pred[1024]{0:T(1024)(128)(4,1)S(1)} %broadcast_compare_fusion, bf16[1,512,1024]{2,1,0:T(8,128)(2,1)S(1)} %copy-done, f32[1024,512]{1,0:T(8,128)} %fusion.2, bf16[1024,1024]{1,0:T(8,128)(2,1)S(1)} %copy-done.1, bf16[1,1024,512]{2,1,0:T(8,128)(2,1)} %param.12), kind=kOutput, calls=%fused_computation | convolution fusion | flops 2152726528 | bytes 10490880 | tf_op jit(solution)/shard_map/dot_general | solution.py:28
  66.6 0.0 reduce-scatter.2.cloned.1.call-update
  66.6 71.6 %reduce-scatter.2.cloned.1.call-done = f32[64,1024]{1,0:T(8,128)} async-done(((f32[1024,1024]{1,0:T(8,128)}), f32[64,1024]{1,0:T(8,128)}) %reduce-scatter.2.cloned.1.call-update) | async-done | bytes 262160 | tf_op jit(solution)/shard_map/reduce_scatter | solution.py:43
  138.2 1.6 %convert_element_type.15 = bf16[64,1024]{1,0:T(8,128)(2,1)} convert(f32[64,1024]{1,0:T(8,128)} %reduce-scatter.2.cloned.1.call-done) | non-fusion elementwise | flops 65536 | bytes 393216 | tf_op jit(solution)/shard_map/convert_element_type | solution.py:44
  (7 shorter events, 0.1 us)
Async XLA Ops:
  6.5 53.8 %copy-start = (bf16[1,512,1024]{2,1,0:T(8,128)(2,1)S(1)}, bf16[1,512,1024]{2,1,0:T(8,128)(2,1)}, u32[]{:S(2)}) copy-start(bf16[1,512,1024]{2,1,0:T(8,128)(2,1)} %param.13) | copy-start | bytes 3145732
  6.5 47.4 %all-gather.3.cloned.1.call-start = ((), (), s32[]{:S(2)}) async-start(), calls=%async_computation.1 | async-start | bytes 2228224 | tf_op jit(solution)/shard_map/all_gather | solution.py:35
  9.4 128.8 %reduce-scatter.2.cloned.1.call-start = ((), (), s32[]{:S(2)}) async-start(), calls=%async_computation.2 | async-start | bytes 4456448 | tf_op jit(solution)/shard_map/reduce_scatter | solution.py:43
  54.0 2.5 %copy-start.1 = (bf16[1024,1024]{1,0:T(8,128)(2,1)S(1)}, bf16[1024,1024]{1,0:T(8,128)(2,1)}, u32[]{:S(2)}) copy-start(bf16[1024,1024]{1,0:T(8,128)(2,1)} %all-gather.3.cloned.1.call-done) | copy-start | bytes 6291460
Sparse Core Ops, SparseCore 0:
  9.5 44.4 all-gather.2
  66.7 71.4 reduce-scatter.1

commit v2 on v1

v2 whole, which is shorter than its diff:
```python
import functools

import jax
import jax.numpy as jnp
from jax import lax
from jax.experimental import pallas as pl
from jax.experimental.pallas import tpu as pltpu
from jax.sharding import PartitionSpec as P

epsilon = 1e-05
LANES = 128
SIDE = 2


def pack_rows(tokens_ref, gain_ref, router_ref, ids_ref):
    values = tokens_ref[...].astype(jnp.float32)
    inverse = lax.rsqrt(jnp.mean(values * values, axis=1, keepdims=True) + epsilon)
    normed = (values * inverse * gain_ref[...]).astype(jnp.bfloat16)
    logits = jnp.dot(normed, router_ref[...], preferred_element_type=jnp.float32)
    top = ids_ref.shape[1]
    numbers = lax.broadcasted_iota(jnp.int32, logits.shape, 1)
    ids = [ids_ref[:, k:k + 1] for k in range(top)]
    chosen = [jnp.sum(jnp.where(numbers == one, logits, 0.0), axis=1, keepdims=True) for one in ids]
    peak = functools.reduce(jnp.maximum, chosen)
    powers = [jnp.exp(one - peak) for one in chosen]
    total = sum(powers[1:], powers[0])
    lane = lax.broadcasted_iota(jnp.int32, (normed.shape[0], LANES), 1)
    extra = jnp.zeros((normed.shape[0], LANES), jnp.float32)
    for k in range(top):
        extra = jnp.where(lane == k, ids[k].astype(jnp.float32), extra)
        rest = powers[k] / total
        for piece in range(3):
            rounded = rest.astype(jnp.bfloat16).astype(jnp.float32)
            extra = jnp.where(lane == (piece + 1) * top + k, rounded, extra)
            rest = rest - rounded
    return normed, extra.astype(jnp.bfloat16)


def kernel(count, top, tokens_ref, gain_ref, router_ref, ids_ref, gate_hbm, up_hbm, down_hbm, out_ref,
           rows, part, from_core, from_x, from_z, w_gate, w_up, w_down,
           w_sem, ag_z_send, ag_z_recv, ag_x_send, ag_x_recv, ag_c_send, ag_c_recv,
           rs_c_send, rs_c_recv, rs_x_send, rs_x_recv, rs_z_send, rs_z_recv):
    planes = count // (SIDE * SIDE)
    me = lax.axis_index("ep")
    z, x, c = me // (SIDE * SIDE), (me // SIDE) % SIDE, me % SIDE
    local = w_gate.shape[0]
    width = out_ref.shape[1]

    def device(pz, px, pc):
        return {"ep": (pz * SIDE + px) * SIDE + pc}

    def remote(src, dst, send, recv, target):
        return pltpu.make_async_remote_copy(src_ref=src, dst_ref=dst, send_sem=send, recv_sem=recv,
                                            device_id=target, device_id_type=pl.DeviceIdType.MESH)

    x_mate, c_mate = device(z, 1 - x, c), device(z, x, 1 - c)
    z_up = [device((z + k) % planes, x, c) for k in range(planes)]
    source = [(z + planes - k) % planes for k in range(planes)]

    weights = [pltpu.make_async_copy(a, b, w_sem.at[i]) for i, (a, b) in
               enumerate([(gate_hbm, w_gate), (up_hbm, w_up), (down_hbm, w_down)])]
    for one in weights:
        one.start()
    barrier = pltpu.get_barrier_semaphore()
    for target in [x_mate, c_mate] + z_up[1:]:
        pl.semaphore_signal(barrier, inc=1, device_id=target, device_id_type=pl.DeviceIdType.MESH)
    normed, extra = pack_rows(tokens_ref, gain_ref, router_ref, ids_ref)
    rows[z, c, x, :, :width] = normed
    rows[z, c, x, :, width:] = extra
    pl.semaphore_wait(barrier, planes + 1)

    sends = []

    def go(copy):
        copy.start()
        sends.append(copy)
        return copy

    def block(k, px, pc):
        return rows.at[source[k], pc, px]

    ag_z = [None] + [go(remote(rows.at[z, c, x], rows.at[z, c, x], ag_z_send.at[k], ag_z_recv.at[k], z_up[k]))
                     for k in range(1, planes)]

    def ag_x(k):
        return remote(block(k, x, c), block(k, x, c), ag_x_send.at[k], ag_x_recv.at[k], x_mate)

    def ag_c(k, j):
        px = x if j == 0 else 1 - x
        return remote(block(k, px, c), block(k, px, c), ag_c_send.at[k, j], ag_c_recv.at[k, j], c_mate)

    def stage_a(k):
        if k:
            remote(block(k, x, c), block(k, x, c), ag_z_send.at[k], ag_z_recv.at[k], z_up[k]).wait_recv()
        go(ag_x(k))
        go(ag_c(k, 0))

    def stage_b(k):
        remote(block(k, 1 - x, c), block(k, 1 - x, c), ag_x_send.at[k], ag_x_recv.at[k], x_mate).wait_recv()
        go(ag_c(k, 1))

    def rs_c(k):
        return remote(part.at[k, 1 - c], from_core.at[k], rs_c_send.at[k], rs_c_recv.at[k], c_mate)

    def rs_x(k):
        return remote(part.at[k, c, 1 - x], from_x.at[k], rs_x_send.at[k], rs_x_recv.at[k], x_mate)

    def rs_z(k):
        return remote(part.at[k, c, x], from_z.at[k], rs_z_send.at[k], rs_z_recv.at[k], device(source[k], x, c))

    def stage_c(k):
        for j in range(SIDE):
            px = x if j == 0 else 1 - x
            remote(block(k, px, 1 - c), block(k, px, 1 - c), ag_c_send.at[k, j], ag_c_recv.at[k, j],
                   c_mate).wait_recv()
        if k == 0:
            for one in weights:
                one.wait()
        held = rows[source[k]].reshape(-1, width + LANES)
        data, extra = held[:, :width], held[:, width:].astype(jnp.float32)
        total = None
        for within in range(local):
            expert = (me * local + within).astype(jnp.float32)
            gate_part = jnp.dot(data, w_gate[within], preferred_element_type=jnp.float32)
            up_part = jnp.dot(data, w_up[within], preferred_element_type=jnp.float32)
            hidden = (gate_part / (1.0 + jnp.exp(-gate_part)) * up_part).astype(jnp.bfloat16)
            produced = jnp.dot(hidden, w_down[within], preferred_element_type=jnp.float32)
            weight = jnp.zeros((held.shape[0], 1), jnp.float32)
            for i in range(top):
                gate = sum(extra[:, (p + 1) * top + i:(p + 1) * top + i + 1] for p in range(3))
                weight = weight + jnp.where(extra[:, i:i + 1] == expert, gate, 0.0)
            term = produced * weight
            total = term if total is None else total + term
        part[k] = total.reshape(part.shape[1:])
        go(rs_c(k))

    def stage_d(k):
        rs_c(k).wait_recv()
        part[k, c, 1 - x] = part[k, c, 1 - x] + from_core[k, 1 - x]
        go(rs_x(k))
        part[k, c, x] = part[k, c, x] + from_core[k, x]

    def stage_e(k):
        rs_x(k).wait_recv()
        part[k, c, x] = part[k, c, x] + from_x[k]
        if k:
            go(rs_z(k))

    stages = {"a": stage_a, "b": stage_b, "c": stage_c, "d": stage_d, "e": stage_e}
    lag = {"b": 0, "a": 1, "c": 0, "d": 0, "e": -2}
    stage_a(0)
    for t in range(planes + 2):
        for name, shift in lag.items():
            if 0 <= t + shift < planes and (name != "a" or t + shift):
                stages[name](t + shift)
    total = part[0, c, x]
    for k in range(1, planes):
        rs_z(k).wait_recv()
        total = total + from_z[k]
    out_ref[...] = total.astype(out_ref.dtype)
    for copy in sends:
        copy.wait_send()


def solution(mesh):
    count = mesh.shape["ep"]

    def shards(tokens, norm_gain, router_weight, expert_ids, w_gate, w_up, w_down):
        size, width = tokens.shape
        planes = count // (SIDE * SIDE)
        top = expert_ids.shape[1]
        dma = pltpu.SemaphoreType.DMA
        vmem = pl.BlockSpec(memory_space=pltpu.VMEM)
        anywhere = pl.BlockSpec(memory_space=pl.ANY)
        f32 = jnp.float32
        return pl.pallas_call(
            functools.partial(kernel, count, top),
            out_shape=jax.ShapeDtypeStruct((size, width), jnp.bfloat16),
            in_specs=[vmem] * 4 + [anywhere] * 3,
            out_specs=vmem,
            scratch_shapes=[
                pltpu.VMEM((planes, SIDE, SIDE, size, width + LANES), jnp.bfloat16),
                pltpu.VMEM((planes, SIDE, SIDE, size, width), f32),
                pltpu.VMEM((planes, SIDE, size, width), f32),
                pltpu.VMEM((planes, size, width), f32),
                pltpu.VMEM((planes, size, width), f32),
                pltpu.VMEM(w_gate.shape, w_gate.dtype),
                pltpu.VMEM(w_up.shape, w_up.dtype),
                pltpu.VMEM(w_down.shape, w_down.dtype),
                dma((3,)), dma((planes,)), dma((planes,)), dma((planes,)), dma((planes,)),
                dma((planes, SIDE)), dma((planes, SIDE)),
                dma((planes,)), dma((planes,)), dma((planes,)), dma((planes,)), dma((planes,)), dma((planes,)),
            ],
            compiler_params=pltpu.CompilerParams(collective_id=0, has_side_effects=True,
                                                 vmem_limit_bytes=60 * 1024 * 1024),
        )(tokens, norm_gain.reshape(1, width), router_weight, expert_ids, w_gate, w_up, w_down)

    return jax.shard_map(
        shards,
        mesh=mesh,
        in_specs=(
            P(("dp", "ep"), None),
            P(),
            P(),
            P(("dp", "ep"), None),
            P("ep", None, None),
            P("ep", None, None),
            P("ep", None, None),
        ),
        out_specs=P(("dp", "ep"), None),
        check_vma=False,
    )
```

time: 147 us -> 72.4 us (0.49)
  waiting for transfers between devices: 92.7 us -> 0 us
  Pallas kernels: 0 us -> 68.3 us
  blocking collectives: 23.4 us -> 0 us
  between operations: 13.5 us -> 0.01 us
  matrix products: 12.5 us -> 0 us
  other arithmetic: 4.49 us -> 0 us
  local copies, waits for them, and re-layouts: 0.1 us -> 3.78 us
    reduce_scatter x1 -> x0, waiting for transfers between devices: 71.6 us -> none  [shards(): finished = lax.psum_scatter(total, 'ep', scatter_dimension=0, tiled=True)]
    pallas_call x0 -> x1, Pallas kernels: none -> 68.3 us  [shards(): pl.pallas_call(functools.partial(kernel, count, top), out_shape=jax.Shape...]
    all_gather x1 -> x0, blocking collectives: 23.4 us -> none  [shards(): all_ids = lax.all_gather(expert_ids, 'ep', axis=0, tiled=True)]
    all_gather x1 -> x0, waiting for transfers between devices: 21 us -> none  [shards(): all_rows = lax.all_gather(normed, 'ep', axis=0, tiled=True)]
    dot_general x3 -> x0, matrix products: 12.5 us -> none  [the longest x1 6.28 us: expert_output(): return jnp.dot(hidden, down_matrix, preferred_element_type=jnp.float32)]
    unnamed x5 -> x7, local copies, waits for them, and re-layouts: 0.09 us -> 3.78 us
    convert_element_type x2 -> x0, other arithmetic: 3.29 us -> none  [the longest x1 1.67 us: normalize(): return (values * inverse * norm_gain).astype(jnp.bfloat16)]
  transfers between devices with their start and end apart: 2 -> 0, of which waited for: 2 -> 0; matrix products, arithmetic and copies ran while one was open for 0% -> 0% of each run, Pallas kernels for 0% -> 0%
where the time goes in v2:
time: 72.4 us; the launch traced here: 72 us
  Pallas kernels  68.3 us (94%)
  local copies, waits for them, and re-layouts  3.78 us (5%)
    pallas_call x1, Pallas kernels, shards(): pl.pallas_call(functools.partial(kernel, count, top), out_shape=jax.Shape...  68.3 us
    unnamed x7, local copies, waits for them, and re-layouts  3.78 us

profile of v2, /device:TPU:0, one launch (start us, length us, event | category | flops | bytes accessed | tf_op | source)
XLA Modules:
  0.0 72.0 jit_solution(3641537230351674962)
XLA Ops:
  0.0 0.0 copy-start.1
  0.0 0.0 copy-start
  0.0 0.7 copy-done.1
  0.7 0.7 copy.9.ids_ref
  1.4 0.0 copy-done
  1.4 0.8 %copy.8.router_ref = bf16[1024,16]{1,0:T(8,128)(2,1)} copy(bf16[1024,16]{0,1:T(8,128)(2,1)S(1)} %copy-done) | data formatting | bytes 65536 | tf_op args[2]
  2.2 68.3 %shard_map.73 = bf16[64,1024]{1,0:T(8,128)(2,1)} custom-call(bf16[64,1024]{1,0:T(8,128)(2,1)} %tokens_ref.1, f32[1,1024]{1,0:T(1,128)} %bitcast.1, bf16[1024,16]{1,0:T(8,128)(2,1)} %copy.8.router_ref, s32[64,2]{1,0:T(8,128)} %copy.9.ids_ref, bf16[1,1024,512]{2,1,0:T(8,128)(2,1)} %gate_hbm.1, bf16[1,1024,512]{2,1,0:T(8,128)(2,1)} %up_hbm.1, ...), custom_call_target="tpu_custom_call" | custom-call | tf_op jit(solution)/shard_map/pallas_call | solution.py:176
  70.5 1.6 %copy.11 = bf16[64,1024]{1,0:T(8,128)(2,1)} copy(bf16[64,1024]{1,0:T(8,128)(2,1)} %shard_map.73) | data formatting | bytes 262144
Async XLA Ops:
  0.0 0.7 copy-start.1
  0.0 1.4 %copy-start = (bf16[1024,16]{0,1:T(8,128)(2,1)S(1)}, bf16[1024,16]{0,1:T(8,128)(2,1)}, u32[]{:S(2)}) copy-start(bf16[1024,16]{0,1:T(8,128)(2,1)} %param.9) | copy-start | bytes 98308

commit v3 on v2

--- a/solution.py
+++ b/solution.py
@@ -146,13 +146,23 @@
         if k:
             go(rs_z(k))
 
-    stages = {"a": stage_a, "b": stage_b, "c": stage_c, "d": stage_d, "e": stage_e}
-    lag = {"b": 0, "a": 1, "c": 0, "d": 0, "e": -2}
     stage_a(0)
-    for t in range(planes + 2):
-        for name, shift in lag.items():
-            if 0 <= t + shift < planes and (name != "a" or t + shift):
-                stages[name](t + shift)
+    stage_b(0)
+    stage_c(0)
+    if planes > 1:
+        stage_a(1)
+    for k in range(1, planes):
+        if k + 1 < planes:
+            stage_a(k + 1)
+        stage_b(k)
+        stage_c(k)
+        stage_d(k)
+        if k > 1:
+            stage_e(k - 1)
+    stage_d(0)
+    if planes > 1:
+        stage_e(planes - 1)
+    stage_e(0)
     total = part[0, c, x]
     for k in range(1, planes):
         rs_z(k).wait_recv()

time: 72.4 us -> 64.1 us (0.89)
  Pallas kernels: 68.3 us -> 60.1 us
    pallas_call x1, Pallas kernels: 68.3 us -> 60.1 us  [shards(): pl.pallas_call(functools.partial(kernel, count, top), out_shape=jax.Shape...]
where the time goes in v3:
time: 64.1 us; the launch traced here: 63.9 us
  Pallas kernels  60.1 us (94%)
  local copies, waits for them, and re-layouts  3.78 us (6%)
    pallas_call x1, Pallas kernels, shards(): pl.pallas_call(functools.partial(kernel, count, top), out_shape=jax.Shape...  60.1 us
    unnamed x7, local copies, waits for them, and re-layouts  3.78 us

profile of v3, /device:TPU:0, one launch (start us, length us, event | category | flops | bytes accessed | tf_op | source)
XLA Modules:
  0.0 63.9 jit_solution(7253816492508608327)
XLA Ops:
  0.0 0.0 copy-start.1
  0.0 0.0 copy-start
  0.0 0.7 %copy-done.1 = s32[64,2]{0,1:T(2,128)S(1)} copy-done((s32[64,2]{0,1:T(2,128)S(1)}, s32[64,2]{0,1:T(2,128)}, u32[]{:S(2)}) %copy-start.1) | copy-done | bytes 536
  0.7 0.7 %copy.9.ids_ref = s32[64,2]{1,0:T(8,128)} copy(s32[64,2]{0,1:T(2,128)S(1)} %copy-done.1) | data formatting | bytes 1024 | tf_op args[3]
  1.4 0.0 copy-done
  1.4 0.8 %copy.8.router_ref = bf16[1024,16]{1,0:T(8,128)(2,1)} copy(bf16[1024,16]{0,1:T(8,128)(2,1)S(1)} %copy-done) | data formatting | bytes 65536 | tf_op args[2]
  2.2 60.1 %shard_map.73 = bf16[64,1024]{1,0:T(8,128)(2,1)} custom-call(bf16[64,1024]{1,0:T(8,128)(2,1)} %tokens_ref.1, f32[1,1024]{1,0:T(1,128)} %bitcast.1, bf16[1024,16]{1,0:T(8,128)(2,1)} %copy.8.router_ref, s32[64,2]{1,0:T(8,128)} %copy.9.ids_ref, bf16[1,1024,512]{2,1,0:T(8,128)(2,1)} %gate_hbm.1, bf16[1,1024,512]{2,1,0:T(8,128)(2,1)} %up_hbm.1, ...), custom_call_target="tpu_custom_call" | custom-call | tf_op jit(solution)/shard_map/pallas_call | solution.py:186
  62.3 1.6 %copy.11 = bf16[64,1024]{1,0:T(8,128)(2,1)} copy(bf16[64,1024]{1,0:T(8,128)(2,1)} %shard_map.73) | data formatting | bytes 262144
Async XLA Ops:
  0.0 0.7 %copy-start.1 = (s32[64,2]{0,1:T(2,128)S(1)}, s32[64,2]{0,1:T(2,128)}, u32[]{:S(2)}) copy-start(s32[64,2]{0,1:T(2,128)} %param.10) | copy-start | bytes 1540
  0.0 1.4 %copy-start = (bf16[1024,16]{0,1:T(8,128)(2,1)S(1)}, bf16[1024,16]{0,1:T(8,128)(2,1)}, u32[]{:S(2)}) copy-start(bf16[1024,16]{0,1:T(8,128)(2,1)} %param.9) | copy-start | bytes 98308

commit v4 on v3

--- a/solution.py
+++ b/solution.py
@@ -10,6 +10,7 @@
 epsilon = 1e-05
 LANES = 128
 SIDE = 2
+STEPS = 32000.0
 
 
 def pack_rows(tokens_ref, gain_ref, router_ref, ids_ref):
@@ -36,8 +37,25 @@
     return normed, extra.astype(jnp.bfloat16)
 
 
+def scale_of(exponent):
+    return jnp.exp(exponent * 0.6931471805599453)
+
+
+def encode(ref, values):
+    width = values.shape[1]
+    peak = jnp.maximum(jnp.max(jnp.abs(values), axis=1, keepdims=True), 1e-30)
+    exponent = jnp.ceil(jnp.log(peak) * 1.4426950408889634)
+    ref[:, :width] = jnp.round(values * (STEPS / scale_of(exponent))).astype(jnp.int32).astype(jnp.int16)
+    ref[:, width:] = jnp.broadcast_to(exponent, (values.shape[0], LANES)).astype(jnp.int32).astype(jnp.int16)
+
+
+def decode(ref, width):
+    exponent = ref[:, width:].astype(jnp.int32).astype(jnp.float32)[:, :1]
+    return ref[:, :width].astype(jnp.int32).astype(jnp.float32) * (scale_of(exponent) * (1.0 / STEPS))
+
+
 def kernel(count, top, tokens_ref, gain_ref, router_ref, ids_ref, gate_hbm, up_hbm, down_hbm, out_ref,
-           rows, part, from_core, from_x, from_z, w_gate, w_up, w_down,
+           rows, part, from_core, to_x, from_x, to_z, from_z, w_gate, w_up, w_down,
            w_sem, ag_z_send, ag_z_recv, ag_x_send, ag_x_recv, ag_c_send, ag_c_recv,
            rs_c_send, rs_c_recv, rs_x_send, rs_x_recv, rs_z_send, rs_z_recv):
     planes = count // (SIDE * SIDE)
@@ -103,10 +121,10 @@
         return remote(part.at[k, 1 - c], from_core.at[k], rs_c_send.at[k], rs_c_recv.at[k], c_mate)
 
     def rs_x(k):
-        return remote(part.at[k, c, 1 - x], from_x.at[k], rs_x_send.at[k], rs_x_recv.at[k], x_mate)
+        return remote(to_x.at[k], from_x.at[k], rs_x_send.at[k], rs_x_recv.at[k], x_mate)
 
     def rs_z(k):
-        return remote(part.at[k, c, x], from_z.at[k], rs_z_send.at[k], rs_z_recv.at[k], device(source[k], x, c))
+        return remote(to_z.at[k], from_z.at[k], rs_z_send.at[k], rs_z_recv.at[k], device(source[k], x, c))
 
     def stage_c(k):
         for j in range(SIDE):
@@ -136,15 +154,16 @@
 
     def stage_d(k):
         rs_c(k).wait_recv()
-        part[k, c, 1 - x] = part[k, c, 1 - x] + from_core[k, 1 - x]
+        encode(to_x.at[k], part[k, c, 1 - x] + from_core[k, 1 - x])
         go(rs_x(k))
-        part[k, c, x] = part[k, c, x] + from_core[k, x]
 
     def stage_e(k):
         rs_x(k).wait_recv()
-        part[k, c, x] = part[k, c, x] + from_x[k]
-        if k:
-            go(rs_z(k))
+        whole = part[k, c, x] + from_core[k, x] + decode(from_x.at[k], width)
+        if k == 0:
+            return whole
+        encode(to_z.at[k], whole)
+        go(rs_z(k))
 
     stage_a(0)
     stage_b(0)
@@ -162,11 +181,10 @@
     stage_d(0)
     if planes > 1:
         stage_e(planes - 1)
-    stage_e(0)
-    total = part[0, c, x]
+    total = stage_e(0)
     for k in range(1, planes):
         rs_z(k).wait_recv()
-        total = total + from_z[k]
+        total = total + decode(from_z.at[k], width)
     out_ref[...] = total.astype(out_ref.dtype)
     for copy in sends:
         copy.wait_send()
@@ -192,8 +210,10 @@
                 pltpu.VMEM((planes, SIDE, SIDE, size, width + LANES), jnp.bfloat16),
                 pltpu.VMEM((planes, SIDE, SIDE, size, width), f32),
                 pltpu.VMEM((planes, SIDE, size, width), f32),
-                pltpu.VMEM((planes, size, width), f32),
-                pltpu.VMEM((planes, size, width), f32),
+                pltpu.VMEM((planes, size, width + LANES), jnp.int16),
+                pltpu.VMEM((planes, size, width + LANES), jnp.int16),
+                pltpu.VMEM((planes, size, width + LANES), jnp.int16),
+                pltpu.VMEM((planes, size, width + LANES), jnp.int16),
                 pltpu.VMEM(w_gate.shape, w_gate.dtype),
                 pltpu.VMEM(w_up.shape, w_up.dtype),
                 pltpu.VMEM(w_down.shape, w_down.dtype),

time: 64.1 us -> 55.1 us (0.86)
  Pallas kernels: 60.1 us -> 51.1 us
    pallas_call x1, Pallas kernels: 60.1 us -> 51.1 us  [shards(): pl.pallas_call(functools.partial(kernel, count, top), out_shape=jax.Shape...]
where the time goes in v4:
time: 55.1 us; the launch traced here: 54.9 us
  Pallas kernels  51.1 us (93%)
  local copies, waits for them, and re-layouts  3.78 us (7%)
    pallas_call x1, Pallas kernels, shards(): pl.pallas_call(functools.partial(kernel, count, top), out_shape=jax.Shape...  51.1 us
    unnamed x7, local copies, waits for them, and re-layouts  3.78 us

profile of v4, /device:TPU:0, one launch (start us, length us, event | category | flops | bytes accessed | tf_op | source)
XLA Modules:
  0.0 54.9 jit_solution(2033172312103352298)
XLA Ops:
  0.0 0.0 copy-start.1
  0.0 0.0 copy-start
  0.0 0.7 %copy-done.1 = s32[64,2]{0,1:T(2,128)S(1)} copy-done((s32[64,2]{0,1:T(2,128)S(1)}, s32[64,2]{0,1:T(2,128)}, u32[]{:S(2)}) %copy-start.1) | copy-done | bytes 536
  0.7 0.7 %copy.9.ids_ref = s32[64,2]{1,0:T(8,128)} copy(s32[64,2]{0,1:T(2,128)S(1)} %copy-done.1) | data formatting | bytes 1024 | tf_op args[3]
  1.4 0.0 copy-done
  1.4 0.8 %copy.8.router_ref = bf16[1024,16]{1,0:T(8,128)(2,1)} copy(bf16[1024,16]{0,1:T(8,128)(2,1)S(1)} %copy-done) | data formatting | bytes 65536 | tf_op args[2]
  2.2 51.1 %shard_map.73 = bf16[64,1024]{1,0:T(8,128)(2,1)} custom-call(bf16[64,1024]{1,0:T(8,128)(2,1)} %tokens_ref.1, f32[1,1024]{1,0:T(1,128)} %bitcast.1, bf16[1024,16]{1,0:T(8,128)(2,1)} %copy.8.router_ref, s32[64,2]{1,0:T(8,128)} %copy.9.ids_ref, bf16[1,1024,512]{2,1,0:T(8,128)(2,1)} %gate_hbm.1, bf16[1,1024,512]{2,1,0:T(8,128)(2,1)} %up_hbm.1, ...), custom_call_target="tpu_custom_call" | custom-call | tf_op jit(solution)/shard_map/pallas_call | solution.py:204
  53.3 1.6 %copy.11 = bf16[64,1024]{1,0:T(8,128)(2,1)} copy(bf16[64,1024]{1,0:T(8,128)(2,1)} %shard_map.73) | data formatting | bytes 262144
Async XLA Ops:
  0.0 0.7 %copy-start.1 = (s32[64,2]{0,1:T(2,128)S(1)}, s32[64,2]{0,1:T(2,128)}, u32[]{:S(2)}) copy-start(s32[64,2]{0,1:T(2,128)} %param.10) | copy-start | bytes 1540
  0.0 1.4 %copy-start = (bf16[1024,16]{0,1:T(8,128)(2,1)S(1)}, bf16[1024,16]{0,1:T(8,128)(2,1)}, u32[]{:S(2)}) copy-start(bf16[1024,16]{0,1:T(8,128)(2,1)} %param.9) | copy-start | bytes 98308

commit v5 on v4

--- a/solution.py
+++ b/solution.py
@@ -17,10 +17,12 @@
     values = tokens_ref[...].astype(jnp.float32)
     inverse = lax.rsqrt(jnp.mean(values * values, axis=1, keepdims=True) + epsilon)
     normed = (values * inverse * gain_ref[...]).astype(jnp.bfloat16)
-    logits = jnp.dot(normed, router_ref[...], preferred_element_type=jnp.float32)
-    top = ids_ref.shape[1]
-    numbers = lax.broadcasted_iota(jnp.int32, logits.shape, 1)
-    ids = [ids_ref[:, k:k + 1] for k in range(top)]
+    logits = lax.dot_general(normed, router_ref[...], (((1,), (1,)), ((), ())), preferred_element_type=jnp.float32)
+    top, size = ids_ref.shape
+    diagonal = (lax.broadcasted_iota(jnp.int32, (size, size), 0) == lax.broadcasted_iota(jnp.int32, (size, size), 1))
+    numbers = lax.broadcasted_iota(jnp.int32, logits.shape, 1).astype(jnp.float32)
+    ids = [jnp.sum(jnp.where(diagonal, ids_ref[k:k + 1, :], 0).astype(jnp.float32), axis=1, keepdims=True)
+           for k in range(top)]
     chosen = [jnp.sum(jnp.where(numbers == one, logits, 0.0), axis=1, keepdims=True) for one in ids]
     peak = functools.reduce(jnp.maximum, chosen)
     powers = [jnp.exp(one - peak) for one in chosen]
@@ -28,7 +30,7 @@
     lane = lax.broadcasted_iota(jnp.int32, (normed.shape[0], LANES), 1)
     extra = jnp.zeros((normed.shape[0], LANES), jnp.float32)
     for k in range(top):
-        extra = jnp.where(lane == k, ids[k].astype(jnp.float32), extra)
+        extra = jnp.where(lane == k, ids[k], extra)
         rest = powers[k] / total
         for piece in range(3):
             rounded = rest.astype(jnp.bfloat16).astype(jnp.float32)
@@ -168,16 +170,19 @@
     stage_a(0)
     stage_b(0)
     stage_c(0)
+    for k in range(1, min(3, planes)):
+        stage_a(k)
     if planes > 1:
-        stage_a(1)
+        stage_b(1)
     for k in range(1, planes):
-        if k + 1 < planes:
-            stage_a(k + 1)
-        stage_b(k)
         stage_c(k)
-        stage_d(k)
+        if k + 2 < planes:
+            stage_a(k + 2)
         if k > 1:
             stage_e(k - 1)
+        stage_d(k)
+        if k + 1 < planes:
+            stage_b(k + 1)
     stage_d(0)
     if planes > 1:
         stage_e(planes - 1)
@@ -223,7 +228,7 @@
             ],
             compiler_params=pltpu.CompilerParams(collective_id=0, has_side_effects=True,
                                                  vmem_limit_bytes=60 * 1024 * 1024),
-        )(tokens, norm_gain.reshape(1, width), router_weight, expert_ids, w_gate, w_up, w_down)
+        )(tokens, norm_gain.reshape(1, width), router_weight.T, expert_ids.T, w_gate, w_up, w_down)
 
     return jax.shard_map(
         shards,

time: 55.1 us -> 51.9 us (0.942)
  local copies, waits for them, and re-layouts: 3.78 us -> 1.57 us
  Pallas kernels: 51.1 us -> 50.2 us
    unnamed x7 -> x1, local copies, waits for them, and re-layouts: 3.78 us -> 1.57 us
    pallas_call x1, Pallas kernels: 51.1 us -> 50.2 us  [shards(): pl.pallas_call(functools.partial(kernel, count, top), out_shape=jax.Shape...]
where the time goes in v5:
time: 51.9 us; the launch traced here: 51.7 us
  Pallas kernels  50.2 us (97%)
  local copies, waits for them, and re-layouts  1.57 us (3%)
    pallas_call x1, Pallas kernels, shards(): pl.pallas_call(functools.partial(kernel, count, top), out_shape=jax.Shape...  50.2 us
    unnamed x1, local copies, waits for them, and re-layouts  1.57 us

profile of v5, /device:TPU:0, one launch (start us, length us, event | category | flops | bytes accessed | tf_op | source)
XLA Modules:
  0.0 51.7 jit_solution(10643126761246776519)
XLA Ops:
  0.0 50.2 %shard_map.73 = bf16[64,1024]{1,0:T(8,128)(2,1)} custom-call(bf16[64,1024]{1,0:T(8,128)(2,1)} %tokens_ref.1, f32[1,1024]{1,0:T(1,128)} %bitcast.4, bf16[16,1024]{1,0:T(8,128)(2,1)} %bitcast.3, s32[2,64]{1,0:T(2,128)} %bitcast.5, bf16[1,1024,512]{2,1,0:T(8,128)(2,1)} %gate_hbm.1, bf16[1,1024,512]{2,1,0:T(8,128)(2,1)} %up_hbm.1, bf16[1,512,1024]{2,1,0:T(8,128)(2,1)} %down_hbm.1), custom_call_target="tpu_custom_call" | custom-call | tf_op jit(solution)/shard_map/pallas_call | solution.py:209
  50.2 1.6 %copy.9 = bf16[64,1024]{1,0:T(8,128)(2,1)} copy(bf16[64,1024]{1,0:T(8,128)(2,1)} %shard_map.73) | data formatting | bytes 262144
